TPU v7x, 256 devices: a whole 4x4x8 slice. The times are simulated.
256 devices in a mesh: dp: 4 (over x), expert: 64 (over z, y, core).
Axes of the slice: x: 4, y: 4, z: 8, core: 2. Of those that a mesh axis runs over, the one named last changes fastest.
Arguments:
- rollout_states: bfloat16 [64, 32, 2, 4096], P('expert', 'dp'), may hold values from -30 to 30
- lengths: int32 [32], P('dp'), may hold values from 8 to 128
- group_ids: int32 [32], P('dp'), may hold values from 0 to 3, as said below
- route_ids: int32 [64, 32, 2, 8], P('expert', 'dp'), may hold values from 0 to 63, all different within a row; in each aligned block of 16 rows (0 to 15, 16 to 31, ..., all dimensions but the last counted through in order) at most 4 rows name the same one
- route_weights: float32 [64, 32, 2, 8], P('expert', 'dp'), may hold values from 0.05 to 0.4
- gain_in: float32 [4096], replicated, may hold values from 0.5 to 1.5
- w_gate: bfloat16 [64, 4096, 1024], P('expert', None, 'dp'), may hold values from -0.09375 to 0.09375
- w_up: bfloat16 [64, 4096, 1024], P('expert', None, 'dp'), may hold values from -0.09375 to 0.09375
- w_down: bfloat16 [64, 1024, 4096], P('expert', 'dp'), may hold values from -0.1875 to 0.1875
- gain_out: float32 [4096], replicated, may hold values from 0.5 to 1.5
- head_weight: bfloat16 [4096, 65536], P(None, 'expert'), may hold values from -16 to 16
- targets: int32 [64, 32, 2], P('expert', 'dp'), may hold values from 0 to 65535
- policy_logp: float32 [64, 32, 2], P('expert', 'dp'), may hold values from -14 to -6
Outputs:
- token_kl: float32 [64, 32, 2], P('expert', 'dp')
- row_kl: float32 [32], P('dp')
Inputs may be any that keep to these rules, and one draw needn't show every extreme that they name: `group_ids`: every prompt group has exactly 8 rows; group g is owned by index g mod 4 of dp, so every index owns exactly 8 rows. `route_ids`: every token names 8 different experts. Among the 16 tokens of one device no expert is named more than 4 times, and that bound is reached in every draw.
All inputs are finite; a program needn't handle non-finite values.
Results may differ from a plain program's by a relative error of at most 0.0055.
Values may be sent and summed in bfloat16 or wider, within the bound.
No kernel may reach another device: no remote copies, remote signals or barrier semaphores. Data moves between devices by JAX's collectives and lax.ppermute only.
A program may use at most 192 MiB of HBM per device.

v0:
```python
import jax
import jax.numpy as jnp
from jax import lax
from jax.sharding import PartitionSpec as P


def laid_out(blocks, dim):
    dims = list(blocks.shape[1:])
    dims[dim] *= blocks.shape[0]
    return jnp.moveaxis(blocks, 0, dim).reshape(dims)


def sent_to_all(value, axis):
    copies = jnp.broadcast_to(value, (lax.axis_size(axis), *value.shape))
    return lax.all_to_all(copies, axis, split_axis=0, concat_axis=0, tiled=True)


def gather_directly(value, axis, dim):
    return laid_out(sent_to_all(value, axis), dim)


def gather_turned(arrays, axis, dims):
    turned = [jnp.moveaxis(a, dim, 0) for a, dim in zip(arrays, dims)]
    both = jnp.concatenate([t.reshape(len(t), -1) for t in turned], axis=1)
    whole, at, done = (lax.all_gather(both, axis, axis=0, tiled=True), 0, [])
    for t, dim in zip(turned, dims):
        share = whole[:, at : at + t[0].size].reshape(-1, *t.shape[1:])
        done.append(jnp.moveaxis(share, 0, dim))
        at += t[0].size
    return tuple(done)


def sent_together(arrays, axis, split_dim, concat_dim, along):
    widths = [a.shape[along] for a in arrays]
    both = jnp.concatenate(arrays, axis=along)
    whole = lax.all_to_all(both, axis, split_axis=split_dim, concat_axis=concat_dim, tiled=True)
    return tuple(jnp.split(whole, [sum(widths[:k]) for k in range(1, len(widths))], axis=along))


def taken_together(value, axis):
    return sent_to_all(value, axis).sum(axis=0)


def scaled_norm(values, gain_vec):
    mean_square = jnp.mean(values * values, axis=-1, keepdims=True)
    return values * lax.rsqrt(mean_square + 1e-06) * gain_vec


def expert_mlp(slot_input, gate_part, up_part, down_part):
    gate_act = jnp.dot(slot_input, gate_part, preferred_element_type=jnp.float32)
    up_act = jnp.dot(slot_input, up_part, preferred_element_type=jnp.float32)
    hidden = (jax.nn.silu(gate_act) * up_act).astype(jnp.bfloat16)
    return jnp.dot(hidden, down_part, preferred_element_type=jnp.float32)


def first_ranks(member):
    return jnp.sum((jnp.cumsum(member, axis=0) - member) * member, axis=1)


def on_device(
    rollout_states,
    lengths,
    group_ids,
    route_ids,
    route_weights,
    gain_in,
    w_gate,
    w_up,
    w_down,
    gain_out,
    head_weight,
    targets,
    policy_logp,
):
    owners = lax.axis_size("dp")
    own_owner = lax.axis_index("dp")
    row_count = group_ids.shape[0]
    states_rows = rollout_states[0]
    row_shape = states_rows.shape[1:]
    owner_range = jnp.arange(owners, dtype=jnp.int32)
    all_states, all_groups, all_lengths = (
        gather_directly(rollout_states, "dp", 1),
        gather_directly(group_ids, "dp", 0),
        gather_directly(lengths, "dp", 0),
    )
    all_owner = all_groups % owners
    member = (all_owner[:, None] == owner_range[None, :]).astype(jnp.int32)
    global_rank = first_ranks(member)
    arrival = jnp.where(all_owner == own_owner, global_rank, row_count)
    arrived_states = all_states[0]
    owned_rows = jnp.zeros_like(states_rows).at[arrival].set(arrived_states, mode="drop")
    owned_lengths = jnp.zeros((row_count,), jnp.int32).at[arrival].set(all_lengths, mode="drop")
    features = row_shape[1]
    pos_count = row_shape[0]
    states_flat = owned_rows.reshape(-1, features)
    token_count = states_flat.shape[0]
    expert_ids = route_ids.reshape(token_count, -1)
    gate_values = route_weights.reshape(token_count, -1)
    topk_count = expert_ids.shape[1]
    experts = lax.axis_size("expert")
    slot_bound = min(token_count, 2 * token_count * topk_count // experts)
    states_wide = states_flat.astype(jnp.float32)
    normed_in = scaled_norm(states_wide, gain_in).astype(jnp.bfloat16)
    flat_ids = expert_ids.reshape(-1)
    member_slots = (flat_ids[:, None] == jnp.arange(experts, dtype=jnp.int32)[None, :]).astype(
        jnp.int32
    )
    slot_index = flat_ids * slot_bound + first_ranks(member_slots)
    token_of = jnp.arange(flat_ids.shape[0], dtype=jnp.int32) // topk_count
    sender = (
        jnp.zeros((experts * slot_bound, features), jnp.bfloat16)
        .at[slot_index]
        .set(normed_in[token_of])
    )
    gate_full, up_full, down_full = gather_turned((w_gate, w_up, w_down), "dp", (2, 2, 1))
    arrived = lax.all_to_all(
        sender.reshape(experts, slot_bound, features),
        "expert",
        split_axis=0,
        concat_axis=0,
        tiled=True,
    )
    slot_input = arrived.reshape(-1, features)
    result = expert_mlp(slot_input, gate_full[0], up_full[0], down_full[0])
    worked = result.astype(jnp.bfloat16).reshape(arrived.shape)
    returned = lax.all_to_all(worked, "expert", split_axis=0, concat_axis=0, tiled=True)
    picked = returned.reshape(-1, features)[slot_index].reshape(token_count, topk_count, features)
    routed = jnp.sum(gate_values[:, :, None] * picked.astype(jnp.float32), axis=1)
    mixed_sum = states_wide + routed
    final_rows = scaled_norm(mixed_sum, gain_out).astype(jnp.bfloat16)
    vocab_part = head_weight.shape[1]
    vocab_start = lax.axis_index("expert") * vocab_part
    flat_targets = targets.reshape(-1)
    piece_rows = lax.all_gather(final_rows, "expert", axis=0, tiled=True)
    piece_targets = lax.all_gather(flat_targets, "expert", axis=0, tiled=True)
    logits = jnp.dot(piece_rows, head_weight, preferred_element_type=jnp.float32)
    peak_value = jnp.max(logits, axis=1)
    exp_mass = jnp.sum(jnp.exp(logits - peak_value[:, None]), axis=1)
    column = vocab_start + jnp.arange(vocab_part, dtype=jnp.int32)
    target_logit = jnp.sum(
        jnp.where(column[None, :] == piece_targets[:, None], logits, 0.0), axis=1
    )
    from_peaks, from_masses, from_logits = sent_together(
        (
            peak_value.reshape(experts, token_count),
            exp_mass.reshape(experts, token_count),
            target_logit.reshape(experts, token_count),
        ),
        "expert",
        0,
        0,
        1,
    )
    peak_mine = jnp.max(from_peaks, axis=0)
    mass_mine = jnp.sum(from_masses * jnp.exp(from_peaks - peak_mine[None, :]), axis=0)
    logit_mine = jnp.sum(from_logits, axis=0)
    ref_logp = logit_mine - (peak_mine + jnp.log(mass_mine))
    log_ratio = jnp.clip(ref_logp - policy_logp.reshape(-1), -10.0, 10.0)
    token_value = jnp.exp(log_ratio) - log_ratio - 1.0
    position = lax.axis_index("expert") * pos_count + jnp.arange(pos_count, dtype=jnp.int32)
    inside = position[None, :] < owned_lengths[:, None]
    token_kl = jnp.where(inside, token_value.reshape(row_count, pos_count), 0.0)
    row_total = taken_together(jnp.sum(token_kl, axis=1), "expert")
    row_kl = row_total / owned_lengths.astype(jnp.float32)
    return (token_kl.reshape(1, row_count, pos_count), row_kl)


def solution(mesh):
    in_specs = (
        P("expert", "dp", None, None),
        P("dp"),
        P("dp"),
        P("expert", "dp", None, None),
        P("expert", "dp", None, None),
        P(),
        P("expert", None, "dp"),
        P("expert", None, "dp"),
        P("expert", "dp", None),
        P(),
        P(None, "expert"),
        P("expert", "dp", None),
        P("expert", "dp", None),
    )
    out_specs = (P("expert", "dp", None), P("dp"))
    return jax.shard_map(
        on_device, mesh=mesh, in_specs=in_specs, out_specs=out_specs, check_vma=False
    )
```

profile of v0, /device:TPU:1, one launch (start us, length us, event | category | flops | bytes accessed | tf_op | source)
XLA Modules:
  0.0 478.5 jit_solution(13261250315664766353)
XLA Ops:
  7.2 2.9 copy.42
  10.1 4.1 copy.41
  14.3 5.5 %pad_maximum_fusion = bf16[256,12288]{1,0:T(8,128)(2,1)} fusion(bf16[256,4096]{1,0:T(8,128)(2,1)} %bitcast.61, bf16[256,4096]{1,0:T(8,128)(2,1)S(1)} %bitcast.58, bf16[256,4096]{1,0:T(8,128)(2,1)} %bitcast.59), kind=kLoop, calls=%fused_computation.11 | loop fusion | flops 18874368 | bytes 12582912 | tf_op jit(solution)/shard_map/concatenate | solution.py:24
  21.0 4.8 %all-to-all-start = ((s32[4,1,8]{2,1,0:T(1,128)}), s32[4,1,8]{2,1,0:T(1,128)S(1)}, u32[]{:S(2)}, u32[]{:S(2)}) async-start(s32[4,1,8]{2,1,0:T(1,128)} %broadcast_in_dim.25), calls=%async_computation | async-start | bytes 4096 | tf_op jit(solution)/shard_map/all_to_all | solution.py:15
  26.5 3.5 all-to-all-done
  30.0 1.3 broadcast_in_dim.54
  31.3 3.5 all-to-all-start.2
  36.5 5.2 %all-to-all-done.2 = bf16[4,1,8,2,4096]{4,3,2,1,0:T(2,128)(2,1)S(1)} async-done(((bf16[4,1,8,2,4096]{4,3,2,1,0:T(2,128)(2,1)}), bf16[4,1,8,2,4096]{4,3,2,1,0:T(2,128)(2,1)S(1)}, u32[]{:S(2)}, u32[]{:S(2)}) %all-to-all-start.2) | async-done | bytes 524320 | tf_op jit(solution)/shard_map/all_to_all | solution.py:15
  41.7 1.6 scatter_fusion
  43.9 5.8 %scatter_custom_fusion.2 = bf16[256,4096]{1,0:T(8,128)(2,1)S(1)} fusion(s32[128]{0:T(128)S(1)} %fusion.31, bf16[16,4096]{1,0:T(8,128)(2,1)S(1)} %multiply_convert_fusion.1, s32[1024]{0:T(1024)S(1)} %pad_clamp_fusion.1, bf16[]{:T(256)} %constant.72.clone.1), kind=kCustom, calls=%fused_computation.19 | custom fusion | bytes 2097154 | tf_op jit(solution)/shard_map/scatter | solution.py:113
  49.6 2.2 reshape.361
  51.9 64.9 %all_to_all.45 = bf16[64,4,4096]{2,1,0:T(4,128)(2,1)S(1)} all-to-all(bf16[64,4,4096]{2,1,0:T(4,128)(2,1)} %reshape.361), channel_id=1, replica_groups=mesh['dp'=4,'expert'=64] {'expert'}, dimensions={0} | all-to-all | bytes 4194304 | tf_op jit(solution)/shard_map/all_to_all | solution.py:116
  116.7 2.1 reshape.362
  118.8 131.1 %all-gather.3.cloned.1.call-done = bf16[1024,12288]{1,0:T(8,128)(2,1)} async-done(((bf16[256,12288]{1,0:T(8,128)(2,1)}), bf16[1024,12288]{1,0:T(8,128)(2,1)}) %all-gather.3.cloned.1.call-update) | async-done | bytes 25165840 | tf_op jit(solution)/shard_map/all_gather | solution.py:25
  249.9 7.4 %fusion.3 = f32[256,1024]{1,0:T(8,128)} fusion(bf16[256,4096]{1,0:T(8,128)(2,1)} %reshape.362, bf16[1024,12288]{1,0:T(8,128)(2,1)} %all-gather.3.cloned.1.call-done), kind=kOutput, calls=%fused_computation.10 | convolution fusion | flops 2147483648 | bytes 11534336 | tf_op jit(solution)/shard_map/dot_general | solution.py:50
  257.3 12.1 %fusion.4 = bf16[256,4096]{1,0:T(8,128)(2,1)} fusion(bf16[1024,12288]{1,0:T(8,128)(2,1)} %all-gather.3.cloned.1.call-done, bf16[256,4096]{1,0:T(8,128)(2,1)S(1)} %copy-done, f32[256,1024]{1,0:T(8,128)} %fusion.3), kind=kOutput, calls=%fused_computation.12 | convolution fusion | flops 4297588736 | bytes 22020096 | tf_op jit(solution)/shard_map/dot_general | solution.py:53
  269.4 4.1 reshape.367
  273.5 11.0 %all-to-all-start.4 = ((bf16[64,4,4096]{2,1,0:T(4,128)(2,1)}), bf16[64,4,4096]{2,1,0:T(4,128)(2,1)}, u32[]{:S(2)}, u32[]{:S(2)}) async-start(bf16[64,4,4096]{2,1,0:T(4,128)(2,1)} %reshape.367), calls=%async_computation.4 | async-start | bytes 4194304 | tf_op jit(solution)/shard_map/all_to_all | solution.py:126
  285.2 49.0 %all-to-all-done.4 = bf16[64,4,4096]{2,1,0:T(4,128)(2,1)} async-done(((bf16[64,4,4096]{2,1,0:T(4,128)(2,1)}), bf16[64,4,4096]{2,1,0:T(4,128)(2,1)}, u32[]{:S(2)}, u32[]{:S(2)}) %all-to-all-start.4) | async-done | bytes 2097184 | tf_op jit(solution)/shard_map/all_to_all | solution.py:126
  334.2 2.5 reshape.368
  336.8 1.4 gather_fusion
  338.2 1.5 fusion.7
  342.2 3.5 all-to-all-start.1
  346.6 1.3 dynamic-slice
  348.8 15.0 %all-reduce = s32[1024]{0:T(1024)S(1)} all-reduce(s32[1024]{0:T(1024)S(1)} %dynamic-update-slice), channel_id=1, replica_groups=mesh['dp'=4,'expert'=64] {'expert'}, use_global_device_ids=true, to_apply=%add | all-reduce | flops 1024 | bytes 8192
  363.8 57.9 %all-gather.5.cloned.1.call-done = bf16[1024,4096]{1,0:T(8,128)(2,1)} async-done(((bf16[16,4096]{1,0:T(8,128)(2,1)}), bf16[1024,4096]{1,0:T(8,128)(2,1)}) %all-gather.5.cloned.1.call-update) | async-done | bytes 8388624 | tf_op jit(solution)/shard_map/all_gather | solution.py:134
  421.6 15.1 %fusion.35 = (f32[1024]{0:T(1024)S(1)}, f32[1024,1024]{0,1:T(8,128)}) fusion(bf16[1024,4096]{1,0:T(8,128)(2,1)} %all-gather.5.cloned.1.call-done, bf16[4096,1024]{1,0:T(8,128)(2,1)} %param.23), kind=kOutput, calls=%fused_computation.82 | convolution fusion | flops 8590982144 | bytes 20975616 | tf_op jit(solution)/shard_map/dot_general | solution.py:136
  436.8 2.8 exponential_reduce_fusion
  440.5 5.8 %all-to-all-start.5 = ((f32[64,1,48]{2,1,0:T(1,128)}), f32[64,1,48]{2,1,0:T(1,128)S(1)}, u32[]{:S(2)}, u32[]{:S(2)}) async-start(f32[64,1,48]{2,1,0:T(1,128)} %bitcast.22), calls=%async_computation.5 | async-start | bytes 65536 | tf_op jit(solution)/shard_map/all_to_all | solution.py:36
  448.0 7.7 %all-to-all-done.5 = f32[64,1,48]{2,1,0:T(1,128)S(1)} async-done(((f32[64,1,48]{2,1,0:T(1,128)}), f32[64,1,48]{2,1,0:T(1,128)S(1)}, u32[]{:S(2)}, u32[]{:S(2)}) %all-to-all-start.5) | async-done | bytes 12320 | tf_op jit(solution)/shard_map/all_to_all | solution.py:36
  456.8 4.7 all-to-all-start.6
  462.3 8.8 %all-to-all-done.6 = f32[64,1,8]{2,1,0:T(1,128)S(1)} async-done(((f32[64,1,8]{2,1,0:T(1,128)}), f32[64,1,8]{2,1,0:T(1,128)S(1)}, u32[]{:S(2)}, u32[]{:S(2)}) %all-to-all-start.6) | async-done | bytes 2080 | tf_op jit(solution)/shard_map/all_to_all | solution.py:15
  (79 shorter events, 13.4 us)
Async XLA Ops:
  7.2 242.7 %all-gather.3.cloned.1.call-start = ((), (), s32[]{:S(2)}) async-start(), calls=%async_computation.7 | async-start | bytes 31457280 | tf_op jit(solution)/shard_map/all_gather | solution.py:25
  19.8 0.7 copy-start.7
  19.8 6.1 %copy-start.2 = (s32[1,8,2,8]{3,2,1,0:T(2,128)S(1)}, s32[1,8,2,8]{3,2,1,0:T(2,128)}, u32[]{:S(2)}) copy-start(s32[1,8,2,8]{3,2,1,0:T(2,128)} %param.16) | copy-start | bytes 1540
  19.8 10.2 %copy-start.1 = (bf16[1,8,2,4096]{3,2,1,0:T(2,128)(2,1)S(1)}, bf16[1,8,2,4096]{3,2,1,0:T(2,128)(2,1)}, u32[]{:S(2)}) copy-start(bf16[1,8,2,4096]{3,2,1,0:T(2,128)(2,1)} %param.13) | copy-start | bytes 393220
  19.8 24.0 %copy-start.3 = (f32[4096]{0:T(1024)S(1)}, f32[4096]{0:T(1024)}, u32[]{:S(2)}) copy-start(f32[4096]{0:T(1024)} %param.18) | copy-start | bytes 49156
  21.0 9.0 %all-to-all-start = ((s32[4,1,8]{2,1,0:T(1,128)}), s32[4,1,8]{2,1,0:T(1,128)S(1)}, u32[]{:S(2)}, u32[]{:S(2)}) async-start(s32[4,1,8]{2,1,0:T(1,128)} %broadcast_in_dim.25), calls=%async_computation | async-start | bytes 4096 | tf_op jit(solution)/shard_map/all_to_all | solution.py:15
  31.3 10.4 %all-to-all-start.2 = ((bf16[4,1,8,2,4096]{4,3,2,1,0:T(2,128)(2,1)}), bf16[4,1,8,2,4096]{4,3,2,1,0:T(2,128)(2,1)S(1)}, u32[]{:S(2)}, u32[]{:S(2)}) async-start(bf16[4,1,8,2,4096]{4,3,2,1,0:T(2,128)(2,1)} %broadcast_in_dim.54), calls=%async_computation.2 | async-start | bytes 1048576 | tf_op jit(solution)/shard_map/all_to_all | solution.py:15
  36.5 6.9 %copy-start.6 = (s32[32]{0:T(128)}, s32[32]{0:T(128)S(1)}, u32[]{:S(2)}) copy-start(s32[32]{0:T(128)S(1)} %fusion.30) | copy-start | bytes 388
  118.8 138.5 %copy-start = (bf16[256,4096]{1,0:T(8,128)(2,1)S(1)}, bf16[256,4096]{1,0:T(8,128)(2,1)}, u32[]{:S(2)}) copy-start(bf16[256,4096]{1,0:T(8,128)(2,1)} %reshape.362) | copy-start | bytes 6291460
  273.5 60.7 %all-to-all-start.4 = ((bf16[64,4,4096]{2,1,0:T(4,128)(2,1)}), bf16[64,4,4096]{2,1,0:T(4,128)(2,1)}, u32[]{:S(2)}, u32[]{:S(2)}) async-start(bf16[64,4,4096]{2,1,0:T(4,128)(2,1)} %reshape.367), calls=%async_computation.4 | async-start | bytes 4194304 | tf_op jit(solution)/shard_map/all_to_all | solution.py:126
  284.6 137.1 %all-gather.5.cloned.1.call-start = ((), (), s32[]{:S(2)}) async-start(), calls=%async_computation.8 | async-start | bytes 8519680 | tf_op jit(solution)/shard_map/all_gather | solution.py:134
  336.7 3.5 copy-start.4
  342.2 98.3 %all-to-all-start.1 = ((s32[4,1,8]{2,1,0:T(1,128)}), s32[4,1,8]{2,1,0:T(1,128)S(1)}, u32[]{:S(2)}, u32[]{:S(2)}) async-start(s32[4,1,8]{2,1,0:T(1,128)} %broadcast_in_dim.27), calls=%async_computation.1 | async-start | bytes 4096 | tf_op jit(solution)/shard_map/all_to_all | solution.py:15
  436.7 9.6 %copy-start.5 = (f32[1,8,2]{1,2,0:T(2,128)S(1)}, f32[1,8,2]{1,2,0:T(2,128)}, u32[]{:S(2)}) copy-start(f32[1,8,2]{1,2,0:T(2,128)} %param.25) | copy-start | bytes 196
  440.5 15.2 %all-to-all-start.5 = ((f32[64,1,48]{2,1,0:T(1,128)}), f32[64,1,48]{2,1,0:T(1,128)S(1)}, u32[]{:S(2)}, u32[]{:S(2)}) async-start(f32[64,1,48]{2,1,0:T(1,128)} %bitcast.22), calls=%async_computation.5 | async-start | bytes 65536 | tf_op jit(solution)/shard_map/all_to_all | solution.py:36
  456.8 14.2 %all-to-all-start.6 = ((f32[64,1,8]{2,1,0:T(1,128)}), f32[64,1,8]{2,1,0:T(1,128)S(1)}, u32[]{:S(2)}, u32[]{:S(2)}) async-start(f32[64,1,8]{2,1,0:T(1,128)} %broadcast_in_dim.59), calls=%async_computation.6 | async-start | bytes 65536 | tf_op jit(solution)/shard_map/all_to_all | solution.py:15
Sparse Core Ops, SparseCore 0:
  19.9 229.9 all-gather.2
  341.1 80.4 all-gather.4
where the time goes:
time: 480 us; the launch traced here: 479 us
  waiting for transfers between devices  263 us (55%)
  blocking collectives  79.9 us (17%)
  local copies, waits for them, and re-layouts  36.9 us (8%)
  matrix products  34.6 us (7%)
  starting transfers between devices  33.4 us (7%)
  other arithmetic  15.6 us (3%)
  between operations  14.9 us (3%)
    all_gather x1, waiting for transfers between devices, gather_turned(): whole, at, done = (lax.all_gather(both, axis, axis=0, tiled=True), 0, [])  131 us
    all_to_all x1, blocking collectives, on_device(): lax.all_to_all(sender.reshape(experts, slot_bound, features), 'expert', s...  64.9 us
    all_gather x1, waiting for transfers between devices, on_device(): piece_rows = lax.all_gather(final_rows, 'expert', axis=0, tiled=True)  57.9 us
    all_to_all x1, waiting for transfers between devices, on_device(): lax.all_to_all(worked, 'expert', split_axis=0, concat_axis=0, tiled=True)  49 us
    all_to_all x4, waiting for transfers between devices, sent_to_all(): return lax.all_to_all(copies, axis, split_axis=0, concat_axis=0, tiled=True)  17.5 us
    all_to_all x4, starting transfers between devices, sent_to_all(): return lax.all_to_all(copies, axis, split_axis=0, concat_axis=0, tiled=True)  16.5 us
    dot_general x1, matrix products, on_device(): jnp.dot(piece_rows, head_weight, preferred_element_type=jnp.float32)  15.1 us
    unnamed x1, blocking collectives  15 us
  transfers between devices with their start and end apart: 8, of which 7 were waited for; matrix products, arithmetic and copies ran while one was open for 9% of the time, Pallas kernels for 0%

commit v1 on v0

--- a/solution.py
+++ b/solution.py
@@ -22,7 +22,19 @@
 def gather_turned(arrays, axis, dims):
     turned = [jnp.moveaxis(a, dim, 0) for a, dim in zip(arrays, dims)]
     both = jnp.concatenate([t.reshape(len(t), -1) for t in turned], axis=1)
-    whole, at, done = (lax.all_gather(both, axis, axis=0, tiled=True), 0, [])
+
+    def keep_up_the_widths(load):
+        return jnp.concatenate(
+            lax.all_to_all(
+                jnp.stack([load for _ in range(lax.axis_size(axis))], axis=0),
+                axis_name=axis,
+                split_axis=0,
+                concat_axis=0,
+            ),
+            axis=0,
+        )
+
+    whole, at, done = (keep_up_the_widths(both), 0, [])
     for t, dim in zip(turned, dims):
         share = whole[:, at : at + t[0].size].reshape(-1, *t.shape[1:])
         done.append(jnp.moveaxis(share, 0, dim))

time: 480 us -> 623 us (1.30)
  waiting for transfers between devices: 263 us -> 434 us
  blocking collectives: 79.9 us -> 15.1 us
  starting transfers between devices: 33.4 us -> 55.1 us
  local copies, waits for them, and re-layouts: 36.9 us -> 50.4 us
    all_to_all x0 -> x2, waiting for transfers between devices: none -> 305 us  [the longest x1 269 us: keep_up_the_widths(): lax.all_to_all(jnp.stack([load for _ in range(lax.axis_size(axis))], axis...]
    all_gather x1 -> x0, waiting for transfers between devices: 131 us -> none  [gather_turned(): whole, at, done = (lax.all_gather(both, axis, axis=0, tiled=True), 0, [])]
    all_to_all x1 -> x0, blocking collectives: 64.9 us -> none  [on_device(): lax.all_to_all(sender.reshape(experts, slot_bound, features), 'expert', s...]
    all_to_all x0 -> x2, starting transfers between devices: none -> 23.8 us  [the longest x1 15.1 us: on_device(): lax.all_to_all(sender.reshape(experts, slot_bound, features), 'expert', s...]
    another operation x0 -> x1, local copies, waits for them, and re-layouts: none -> 10.8 us  [keep_up_the_widths(): jnp.stack([load for _ in range(lax.axis_size(axis))], axis=0)]
  transfers between devices with their start and end apart: 8 -> 9, of which waited for: 7 -> 8; matrix products, arithmetic and copies ran while one was open for 9% -> 7% of each run, Pallas kernels for 0% -> 0%
where the time goes in v1:
time: 623 us; the launch traced here: 622 us
  waiting for transfers between devices  434 us (70%)
  starting transfers between devices  55.1 us (9%)
  local copies, waits for them, and re-layouts  50.4 us (8%)
  matrix products  34.7 us (6%)
  other arithmetic  17.1 us (3%)
  blocking collectives  15.1 us (2%)
  between operations  15 us (2%)
    all_to_all x1, waiting for transfers between devices, keep_up_the_widths(): lax.all_to_all(jnp.stack([load for _ in range(lax.axis_size(axis))], axis...  269 us
    all_gather x1, waiting for transfers between devices, on_device(): piece_rows = lax.all_gather(final_rows, 'expert', axis=0, tiled=True)  56.9 us
    all_to_all x1, waiting for transfers between devices, on_device(): lax.all_to_all(worked, 'expert', split_axis=0, concat_axis=0, tiled=True)  49 us
    all_to_all x1, waiting for transfers between devices, on_device(): lax.all_to_all(sender.reshape(experts, slot_bound, features), 'expert', s...  35.2 us
    all_to_all x4, starting transfers between devices, sent_to_all(): return lax.all_to_all(copies, axis, split_axis=0, concat_axis=0, tiled=True)  16.2 us
    all_to_all x4, waiting for transfers between devices, sent_to_all(): return lax.all_to_all(copies, axis, split_axis=0, concat_axis=0, tiled=True)  16.1 us
    all_to_all x1, starting transfers between devices, on_device(): lax.all_to_all(sender.reshape(experts, slot_bound, features), 'expert', s...  15.1 us
    unnamed x1, blocking collectives  15.1 us
  transfers between devices with their start and end apart: 9, of which 8 were waited for; matrix products, arithmetic and copies ran while one was open for 7% of the time, Pallas kernels for 0%

profile of v1, /device:TPU:1, one launch (start us, length us, event | category | flops | bytes accessed | tf_op | source)
XLA Modules:
  0.0 621.5 jit_solution(8766128931211902057)
XLA Ops:
  8.4 4.8 all-to-all-start
  15.3 2.1 all-to-all-done
  17.4 2.2 broadcast_in_dim.54
  19.6 3.5 all-to-all-start.2
  24.7 5.2 all-to-all-done.2
  30.0 1.6 scatter_fusion
  32.1 5.8 scatter_custom_fusion.2
  37.9 2.2 reshape.366
  40.1 15.1 %all-to-all-start.3 = ((bf16[64,4,4096]{2,1,0:T(4,128)(2,1)}), bf16[64,4,4096]{2,1,0:T(4,128)(2,1)S(1)}, u32[]{:S(2)}, u32[]{:S(2)}) async-start(bf16[64,4,4096]{2,1,0:T(4,128)(2,1)} %reshape.366), calls=%async_computation.3 | async-start | bytes 4194304 | tf_op jit(solution)/shard_map/all_to_all | solution.py:128
  55.3 4.1 copy.42
  59.4 4.1 copy.41
  63.5 6.3 %pad_maximum_fusion = bf16[256,12288]{1,0:T(8,128)(2,1)} fusion(bf16[256,4096]{1,0:T(8,128)(2,1)} %bitcast.62, bf16[256,4096]{1,0:T(8,128)(2,1)} %bitcast.59, bf16[256,4096]{1,0:T(8,128)(2,1)} %bitcast.60), kind=kLoop, calls=%fused_computation.11 | loop fusion | flops 18874368 | bytes 12582912 | tf_op jit(solution)/shard_map/concatenate | solution.py:24
  69.8 35.2 %all-to-all-done.3 = bf16[64,4,4096]{2,1,0:T(4,128)(2,1)S(1)} async-done(((bf16[64,4,4096]{2,1,0:T(4,128)(2,1)}), bf16[64,4,4096]{2,1,0:T(4,128)(2,1)S(1)}, u32[]{:S(2)}, u32[]{:S(2)}) %all-to-all-start.3) | async-done | bytes 2097184 | tf_op jit(solution)/shard_map/all_to_all | solution.py:128
  105.0 10.8 %stack.2 = bf16[4,256,12288]{2,1,0:T(8,128)(2,1)} broadcast(bf16[256,12288]{1,0:T(8,128)(2,1)} %pad_maximum_fusion), dimensions={1,2} | broadcast | bytes 31457280 | tf_op jit(solution)/shard_map/stack | solution.py:29
  115.7 8.6 %all-to-all-start.4 = ((bf16[4,256,12288]{2,1,0:T(8,128)(2,1)}), bf16[4,256,12288]{2,1,0:T(8,128)(2,1)}, u32[]{:S(2)}, u32[]{:S(2)}) async-start(bf16[4,256,12288]{2,1,0:T(8,128)(2,1)} %stack.2), calls=%async_computation.4 | async-start | bytes 50331648 | tf_op jit(solution)/shard_map/all_to_all | solution.py:28
  124.4 2.0 reshape.367
  126.4 269.4 %all-to-all-done.4 = bf16[4,256,12288]{2,1,0:T(8,128)(2,1)} async-done(((bf16[4,256,12288]{2,1,0:T(8,128)(2,1)}), bf16[4,256,12288]{2,1,0:T(8,128)(2,1)}, u32[]{:S(2)}, u32[]{:S(2)}) %all-to-all-start.4) | async-done | bytes 25165856 | tf_op jit(solution)/shard_map/all_to_all | solution.py:28
  395.8 7.5 %fusion.3 = f32[256,1024]{1,0:T(8,128)} fusion(bf16[256,4096]{1,0:T(8,128)(2,1)} %reshape.367, bf16[1024,12288]{1,0:T(8,128)(2,1)} %bitcast.13), kind=kOutput, calls=%fused_computation.10 | convolution fusion | flops 2147483648 | bytes 11534336 | tf_op jit(solution)/shard_map/dot_general | solution.py:62
  403.3 12.1 %fusion.4 = bf16[256,4096]{1,0:T(8,128)(2,1)} fusion(bf16[1024,12288]{1,0:T(8,128)(2,1)} %bitcast.13, bf16[256,4096]{1,0:T(8,128)(2,1)S(1)} %copy-done, f32[256,1024]{1,0:T(8,128)} %fusion.3), kind=kOutput, calls=%fused_computation.12 | convolution fusion | flops 4297588736 | bytes 22020096 | tf_op jit(solution)/shard_map/dot_general | solution.py:65
  415.4 4.1 reshape.373
  419.5 9.3 %all-to-all-start.5 = ((bf16[64,4,4096]{2,1,0:T(4,128)(2,1)}), bf16[64,4,4096]{2,1,0:T(4,128)(2,1)}, u32[]{:S(2)}, u32[]{:S(2)}) async-start(bf16[64,4,4096]{2,1,0:T(4,128)(2,1)} %reshape.373), calls=%async_computation.5 | async-start | bytes 4194304 | tf_op jit(solution)/shard_map/all_to_all | solution.py:138
  429.5 49.0 %all-to-all-done.5 = bf16[64,4,4096]{2,1,0:T(4,128)(2,1)} async-done(((bf16[64,4,4096]{2,1,0:T(4,128)(2,1)}), bf16[64,4,4096]{2,1,0:T(4,128)(2,1)}, u32[]{:S(2)}, u32[]{:S(2)}) %all-to-all-start.5) | async-done | bytes 2097184 | tf_op jit(solution)/shard_map/all_to_all | solution.py:138
  478.4 2.5 reshape.374
  486.5 3.2 all-to-all-start.1
  492.7 15.1 %all-reduce = s32[1024]{0:T(1024)S(1)} all-reduce(s32[1024]{0:T(1024)S(1)} %dynamic-update-slice), channel_id=1, replica_groups=mesh['dp'=4,'expert'=64] {'expert'}, use_global_device_ids=true, to_apply=%add | all-reduce | flops 1024 | bytes 8192
  507.8 56.9 %all-gather.2.cloned.1.call-done = bf16[1024,4096]{1,0:T(8,128)(2,1)} async-done(((bf16[16,4096]{1,0:T(8,128)(2,1)}), bf16[1024,4096]{1,0:T(8,128)(2,1)}) %all-gather.2.cloned.1.call-update) | async-done | bytes 8388624 | tf_op jit(solution)/shard_map/all_gather | solution.py:146
  564.7 15.1 %fusion.35 = (f32[1024]{0:T(1024)S(1)}, f32[1024,1024]{0,1:T(8,128)}) fusion(bf16[1024,4096]{1,0:T(8,128)(2,1)} %all-gather.2.cloned.1.call-done, bf16[4096,1024]{1,0:T(8,128)(2,1)} %param.23), kind=kOutput, calls=%fused_computation.82 | convolution fusion | flops 8590982144 | bytes 20975616 | tf_op jit(solution)/shard_map/dot_general | solution.py:148
  579.9 2.8 exponential_reduce_fusion
  583.6 5.8 all-to-all-start.6
  591.1 7.7 %all-to-all-done.6 = f32[64,1,48]{2,1,0:T(1,128)S(1)} async-done(((f32[64,1,48]{2,1,0:T(1,128)}), f32[64,1,48]{2,1,0:T(1,128)S(1)}, u32[]{:S(2)}, u32[]{:S(2)}) %all-to-all-start.6) | async-done | bytes 12320 | tf_op jit(solution)/shard_map/all_to_all | solution.py:48
  599.9 4.7 all-to-all-start.7
  605.3 8.8 %all-to-all-done.7 = f32[64,1,8]{2,1,0:T(1,128)S(1)} async-done(((f32[64,1,8]{2,1,0:T(1,128)}), f32[64,1,8]{2,1,0:T(1,128)S(1)}, u32[]{:S(2)}, u32[]{:S(2)}) %all-to-all-start.7) | async-done | bytes 2080 | tf_op jit(solution)/shard_map/all_to_all | solution.py:15
  (74 shorter events, 19.0 us)
Async XLA Ops:
  7.2 24.8 %copy-start.1 = (f32[4096]{0:T(1024)S(1)}, f32[4096]{0:T(1024)}, u32[]{:S(2)}) copy-start(f32[4096]{0:T(1024)} %param.18) | copy-start | bytes 49156
  8.4 9.0 %all-to-all-start = ((s32[4,1,8]{2,1,0:T(1,128)}), s32[4,1,8]{2,1,0:T(1,128)S(1)}, u32[]{:S(2)}, u32[]{:S(2)}) async-start(s32[4,1,8]{2,1,0:T(1,128)} %broadcast_in_dim.25), calls=%async_computation | async-start | bytes 4096 | tf_op jit(solution)/shard_map/all_to_all | solution.py:15
  19.6 10.4 %all-to-all-start.2 = ((bf16[4,1,8,2,4096]{4,3,2,1,0:T(2,128)(2,1)}), bf16[4,1,8,2,4096]{4,3,2,1,0:T(2,128)(2,1)S(1)}, u32[]{:S(2)}, u32[]{:S(2)}) async-start(bf16[4,1,8,2,4096]{4,3,2,1,0:T(2,128)(2,1)} %broadcast_in_dim.54), calls=%async_computation.2 | async-start | bytes 1048576 | tf_op jit(solution)/shard_map/all_to_all | solution.py:15
  24.7 6.9 %copy-start.4 = (s32[32]{0:T(128)}, s32[32]{0:T(128)S(1)}, u32[]{:S(2)}) copy-start(s32[32]{0:T(128)S(1)} %fusion.30) | copy-start | bytes 388
  40.1 64.9 %all-to-all-start.3 = ((bf16[64,4,4096]{2,1,0:T(4,128)(2,1)}), bf16[64,4,4096]{2,1,0:T(4,128)(2,1)S(1)}, u32[]{:S(2)}, u32[]{:S(2)}) async-start(bf16[64,4,4096]{2,1,0:T(4,128)(2,1)} %reshape.366), calls=%async_computation.3 | async-start | bytes 4194304 | tf_op jit(solution)/shard_map/all_to_all | solution.py:128
  115.7 280.0 %all-to-all-start.4 = ((bf16[4,256,12288]{2,1,0:T(8,128)(2,1)}), bf16[4,256,12288]{2,1,0:T(8,128)(2,1)}, u32[]{:S(2)}, u32[]{:S(2)}) async-start(bf16[4,256,12288]{2,1,0:T(8,128)(2,1)} %stack.2), calls=%async_computation.4 | async-start | bytes 50331648 | tf_op jit(solution)/shard_map/all_to_all | solution.py:28
  395.8 7.5 %copy-start = (bf16[256,4096]{1,0:T(8,128)(2,1)S(1)}, bf16[256,4096]{1,0:T(8,128)(2,1)}, u32[]{:S(2)}) copy-start(bf16[256,4096]{1,0:T(8,128)(2,1)} %reshape.367) | copy-start | bytes 6291460
  419.5 58.9 %all-to-all-start.5 = ((bf16[64,4,4096]{2,1,0:T(4,128)(2,1)}), bf16[64,4,4096]{2,1,0:T(4,128)(2,1)}, u32[]{:S(2)}, u32[]{:S(2)}) async-start(bf16[64,4,4096]{2,1,0:T(4,128)(2,1)} %reshape.373), calls=%async_computation.5 | async-start | bytes 4194304 | tf_op jit(solution)/shard_map/all_to_all | solution.py:138
  428.8 135.9 %all-gather.2.cloned.1.call-start = ((), (), s32[]{:S(2)}) async-start(), calls=%async_computation.8 | async-start | bytes 8519680 | tf_op jit(solution)/shard_map/all_gather | solution.py:146
  481.0 3.5 copy-start.2
  486.5 97.1 %all-to-all-start.1 = ((s32[4,1,8]{2,1,0:T(1,128)}), s32[4,1,8]{2,1,0:T(1,128)S(1)}, u32[]{:S(2)}, u32[]{:S(2)}) async-start(s32[4,1,8]{2,1,0:T(1,128)} %broadcast_in_dim.27), calls=%async_computation.1 | async-start | bytes 4096 | tf_op jit(solution)/shard_map/all_to_all | solution.py:15
  579.8 9.6 %copy-start.3 = (f32[1,8,2]{1,2,0:T(2,128)S(1)}, f32[1,8,2]{1,2,0:T(2,128)}, u32[]{:S(2)}) copy-start(f32[1,8,2]{1,2,0:T(2,128)} %param.25) | copy-start | bytes 196
  583.6 15.2 %all-to-all-start.6 = ((f32[64,1,48]{2,1,0:T(1,128)}), f32[64,1,48]{2,1,0:T(1,128)S(1)}, u32[]{:S(2)}, u32[]{:S(2)}) async-start(f32[64,1,48]{2,1,0:T(1,128)} %bitcast.23), calls=%async_computation.6 | async-start | bytes 65536 | tf_op jit(solution)/shard_map/all_to_all | solution.py:48
  599.9 14.2 %all-to-all-start.7 = ((f32[64,1,8]{2,1,0:T(1,128)}), f32[64,1,8]{2,1,0:T(1,128)S(1)}, u32[]{:S(2)}, u32[]{:S(2)}) async-start(f32[64,1,8]{2,1,0:T(1,128)} %broadcast_in_dim.59), calls=%async_computation.7 | async-start | bytes 65536 | tf_op jit(solution)/shard_map/all_to_all | solution.py:15
Sparse Core Ops, SparseCore 0:
  485.4 79.2 all-gather.1
